TPU v7x, 256 devices: a whole 4x4x8 slice. The times are simulated.
256 devices in a mesh: seq: 32 (over y, z), tp: 8 (over x, core).
Axes of the slice: x: 4, y: 4, z: 8, core: 2. Of those that a mesh axis runs over, the one named last changes fastest.
Arguments:
- tokens: bfloat16 [24576, 2048], P('seq', 'tp'), may hold values from -20 to 20
- w_query: bfloat16 [2048, 2048], P(None, 'tp'), may hold values from -0.125 to 0.125
- w_key: bfloat16 [2048, 2048], P(None, 'tp'), may hold values from -0.125 to 0.125
- w_value: bfloat16 [2048, 2048], P(None, 'tp'), may hold values from -0.125 to 0.125
- head_gain: float32 [2048], P('tp'), may hold values from 0.5 to 1.5
- w_out: bfloat16 [2048, 2048], P('tp'), may hold values from -0.125 to 0.125
- norm_gain: float32 [2048], replicated, may hold values from 0.5 to 1.5
- w_gate: bfloat16 [2048, 8192], P('seq', 'tp'), may hold values from -0.125 to 0.125
- w_up: bfloat16 [2048, 8192], P('seq', 'tp'), may hold values from -0.125 to 0.125
- w_down: bfloat16 [8192, 2048], P('tp', 'seq'), may hold values from -0.0625 to 0.0625
Outputs:
- layer_out: bfloat16 [24576, 2048], P('seq', 'tp')
All inputs are finite; a program needn't handle non-finite values.
Results may differ from a plain program's by a relative error of at most 0.009.
Values may be sent and summed in bfloat16 or wider, within the bound.
No kernel may reach another device: no remote copies, remote signals or barrier semaphores. Data moves between devices by JAX's collectives and lax.ppermute only.
A program may use at most 128 MiB of HBM per device.

v0:
```python
import jax
import jax.numpy as jnp
from jax import lax
from jax.sharding import Mesh
from jax.sharding import PartitionSpec as P

HD = 128
SEQ = ("seq_0", "seq_1")


def nothing_yet(array, identity):
    return jnp.zeros_like(array) + jnp.asarray(identity, array.dtype)


def entering(array, axes, combine, identity):
    before = start = nothing_yet(array, identity)
    total = array
    for axis in reversed(axes):
        peers, position = (lax.axis_size(axis), lax.axis_index(axis))
        pieces = lax.all_gather(total.astype(jnp.bfloat16), axis)
        inside, total = (start, start)
        for k in range(peers):
            passed = k < position
            total = combine(total, pieces[k].astype(array.dtype))
            inside = jnp.where(passed, total, inside)
        before = combine(inside, before)
    return before


def in_one_piece(arrays, axis, dim, along):
    ends, at = ([], 0)
    for a in arrays[:-1]:
        at += a.shape[along]
        ends.append(at)
    both = jnp.concatenate(arrays, axis=along)
    return tuple(jnp.split(lax.all_gather(both, axis, axis=dim, tiled=True), ends, axis=along))


def split_up(array, dim, peers):
    shape = array.shape
    tiles = array.reshape(*shape[:dim], peers, shape[dim] // peers, *shape[dim + 1 :])
    return jnp.moveaxis(tiles, dim, 0)


def sum_at_owner(array, axis, dim):
    tiles = split_up(array, dim, lax.axis_size(axis))
    arrived = lax.all_to_all(tiles, axis, split_axis=0, concat_axis=0, tiled=True)
    return arrived.astype(jnp.float32).sum(axis=0)


def add_states(earlier, later):
    return earlier + later


def body(tokens, w_query, w_key, w_value, head_gain, w_out, norm_gain, w_gate, w_up, w_down):
    length = tokens.shape[0]
    width_here = tokens.shape[1]
    heads_here = w_query.shape[1] // HD
    features = lax.all_gather(tokens, "tp", axis=1, tiled=True)

    def project(weight):
        product = jnp.dot(features, weight, preferred_element_type=jnp.float32)
        return product.astype(jnp.bfloat16).reshape(length, heads_here, HD)

    query = project(w_query)
    keys_local = project(w_key)
    values_local = project(w_value)
    scores = jnp.einsum("ihd,jhd->hij", query, keys_local, preferred_element_type=jnp.float32)
    causal = jnp.arange(length)[:, None] >= jnp.arange(length)[None, :]
    scores = jnp.where(causal[None], scores, 0.0).astype(jnp.bfloat16)
    inside = jnp.einsum("hij,jhd->ihd", scores, values_local, preferred_element_type=jnp.float32)
    own_state = jnp.einsum(
        "jhd,jhe->hde", keys_local, values_local, preferred_element_type=jnp.float32
    )
    history = entering(own_state, SEQ, add_states, jnp.zeros_like(own_state))
    carried = jnp.einsum(
        "ihd,hde->ihe", query, history.astype(jnp.bfloat16), preferred_element_type=jnp.float32
    )
    mixed = inside + carried
    scale = lax.rsqrt(jnp.mean(mixed * mixed, axis=-1, keepdims=True) + 1e-06)
    normed = (mixed * scale * head_gain.reshape(heads_here, HD)).astype(jnp.bfloat16)
    normed = normed.reshape(length, heads_here * HD)
    partial_value = jnp.dot(normed, w_out, preferred_element_type=jnp.float32)
    own_column = lax.axis_index("tp") * width_here
    summed = lax.psum(partial_value.astype(jnp.bfloat16), "tp").astype(jnp.float32)
    resid_whole = features.astype(jnp.float32) + summed
    factor = lax.rsqrt(jnp.mean(resid_whole * resid_whole, axis=-1, keepdims=True) + 1e-05)
    ffn_in = (resid_whole * factor * norm_gain).astype(jnp.bfloat16)
    resid = lax.dynamic_slice_in_dim(resid_whole, own_column, width_here, 1)
    pieces = in_one_piece((w_gate, w_up), SEQ, 0, 1)
    gate_sum = jnp.dot(ffn_in, pieces[0], preferred_element_type=jnp.float32)
    upward_sum = jnp.dot(ffn_in, pieces[1], preferred_element_type=jnp.float32)
    hidden = (jax.nn.silu(gate_sum) * upward_sum).astype(jnp.bfloat16)
    terms = jnp.dot(
        hidden, lax.all_gather(w_down, SEQ, axis=1, tiled=True), preferred_element_type=jnp.float32
    )
    mlp_share = sum_at_owner(terms.astype(jnp.bfloat16), "tp", 1)
    return (resid + mlp_share).astype(jnp.bfloat16)


def solution(mesh):
    finer = Mesh(mesh.devices.reshape(4, 8, mesh.shape["tp"]), ("seq_0", "seq_1", "tp"))
    return jax.shard_map(
        body,
        mesh=finer,
        in_specs=(
            P(SEQ, "tp"),
            P(None, "tp"),
            P(None, "tp"),
            P(None, "tp"),
            P("tp"),
            P("tp", None),
            P(),
            P(SEQ, "tp"),
            P(SEQ, "tp"),
            P("tp", SEQ),
        ),
        out_specs=P(SEQ, "tp"),
        check_vma=False,
    )
```

profile of v0, /device:TPU:1, one launch (start us, length us, event | category | flops | bytes accessed | tf_op | source)
XLA Modules:
  0.0 356.1 jit_solution(3774338087254047791)
XLA Ops:
  7.4 0.7 all-gather.5.cloned.1.call-update
  8.2 0.2 iota_compare_fusion
  8.3 39.5 %all-gather.5.cloned.1.call-done = bf16[768,2048]{1,0:T(8,128)(2,1)} async-done(((bf16[768,256]{1,0:T(8,128)(2,1)}), bf16[768,2048]{1,0:T(8,128)(2,1)}) %all-gather.5.cloned.1.call-update) | async-done | bytes 3145744 | tf_op jit(solution)/shard_map/all_gather | solution.py:59
  47.9 3.3 convolution_convert_fusion.2
  51.2 2.4 convolution_convert_fusion.4
  53.6 0.3 convolution_convert_fusion.5
  53.9 20.8 %all-gather = bf16[16,128,128]{2,1,0:T(8,128)(2,1)S(1)} all-gather(bf16[2,128,128]{2,1,0:T(8,128)(2,1)S(1)} %convolution_convert_fusion.5), channel_id=2, replica_groups=mesh['seq_0'=4,'seq_1'=8,'tp'=8] {'seq_1'}, dimensions={0}, use_global_device_ids=true | all-gather | bytes 589824 | tf_op jit(solution)/shard_map/all_gather | solution.py:20
  74.7 0.1 fusion.28
  74.7 9.7 %all_gather.22 = bf16[4,2,128,128]{3,2,1,0:T(8,128)(2,1)S(1)} all-gather(bf16[1,2,128,128]{3,2,1,0:T(8,128)(2,1)S(1)} %fusion.28), channel_id=1, replica_groups=mesh['seq_0'=4,'seq_1'=8,'tp'=8] {'seq_0'}, dimensions={0}, use_global_device_ids=true | all-gather | bytes 327680 | tf_op jit(solution)/shard_map/all_gather | solution.py:20
  84.5 1.1 convolution_convert_fusion.3
  85.6 0.7 copy-done.7
  86.3 1.3 fusion.29
  87.6 2.9 multiply_reduce_fusion.1
  90.5 0.1 multiply_convert_fusion.2
  90.6 2.7 convolution_convert_fusion.1
  93.4 0.0 all-gather.7.cloned.1.call-start
  93.5 0.8 copy-done.2
  94.3 0.1 copy-done.3
  94.3 0.7 pad_maximum_fusion
  95.1 0.2 all-gather.9.cloned.1.call-start
  95.3 0.4 all-gather.9.cloned.1.call-update
  95.7 79.1 %all-reduce.2.cloned.1.call-done = bf16[768,2048]{1,0:T(8,128)(2,1)} async-done(((bf16[768,2048]{1,0:T(8,128)(2,1)}), bf16[768,2048]{1,0:T(8,128)(2,1)}) %all-reduce.2.cloned.1.call-update) | async-done | bytes 3145744 | tf_op jit(solution)/shard_map/psum | solution.py:85
  174.8 6.7 %convert_add_fusion = (f32[768,2048]{1,0:T(8,128)}, f32[768]{0:T(1024)S(1)}) fusion(bf16[768,2048]{1,0:T(8,128)(2,1)} %all-reduce.2.cloned.1.call-done, bf16[768,2048]{1,0:T(8,128)(2,1)} %all-gather.5.cloned.1.call-done), kind=kLoop, calls=%fused_computation.3 | loop fusion | flops 7863552 | bytes 12585984 | tf_op jit(solution)/shard_map/add | solution.py:86
  181.6 19.3 %all-gather.7.cloned.1.call-done = bf16[2048,2048]{1,0:T(8,128)(2,1)} async-done(((bf16[64,2048]{1,0:T(8,128)(2,1)}), bf16[2048,2048]{1,0:T(8,128)(2,1)}) %all-gather.7.cloned.1.call-update) | async-done | bytes 8388624 | tf_op jit(solution)/shard_map/all_gather | solution.py:36
  200.9 9.2 %fusion = f32[768,1024]{1,0:T(8,128)} fusion(bf16[2048,2048]{1,0:T(8,128)(2,1)} %all-gather.7.cloned.1.call-done, f32[2048]{0:T(1024)S(1)} %copy-done.6, f32[768]{0:T(1024)S(1)} %add_rsqrt_fusion.1, bf16[768,2048]{1,0:T(8,128)(2,1)} %all-reduce.2.cloned.1.call-done, bf16[768,2048]{1,0:T(8,128)(2,1)} %all-gather.5.cloned.1.call-done), kind=kOutput, calls=%fused_computation.5 | convolution fusion | flops 3230662656 | bytes 13642752 | tf_op jit(solution)/shard_map/dot_general | solution.py:92
  210.2 69.3 %all-gather.9.cloned.1.call-done = bf16[1024,2048]{0,1:T(8,128)(2,1)} async-done(((bf16[1024,64]{0,1:T(8,128)(2,1)}), bf16[1024,2048]{0,1:T(8,128)(2,1)}) %all-gather.9.cloned.1.call-update) | async-done | bytes 4194320 | tf_op jit(solution)/shard_map/all_gather | solution.py:95
  279.5 14.9 %convolution_convert_fusion = bf16[768,2048]{1,0:T(8,128)(2,1)} fusion(bf16[1024,2048]{0,1:T(8,128)(2,1)} %all-gather.9.cloned.1.call-done, f32[768,1024]{1,0:T(8,128)} %fusion, bf16[2048,2048]{1,0:T(8,128)(2,1)} %all-gather.7.cloned.1.call-done, f32[2048]{0:T(1024)S(1)} %copy-done.6, f32[768]{0:T(1024)S(1)} %add_rsqrt_fusion.1, ...), kind=kOutput, calls=%fused_computation.9 | convolution fusion | flops 6458179584 | bytes 20982784 | tf_op jit(solution)/shard_map/dot_general | solution.py:94
  294.4 3.7 %copy.23 = bf16[96,8,8,256]{3,2,0,1:T(8,128)(2,1)} copy(bf16[96,8,8,256]{3,2,1,0:T(8,128)(2,1)} %bitcast.58) | data formatting | bytes 6291456 | tf_op jit(solution)/shard_map/reshape | solution.py:41
  298.1 8.6 %all-to-all-start = ((bf16[8,768,256]{2,1,0:T(8,128)(2,1)}), bf16[8,768,256]{2,1,0:T(8,128)(2,1)}, u32[]{:S(2)}, u32[]{:S(2)}) async-start(bf16[8,768,256]{2,1,0:T(8,128)(2,1)} %bitcast.57), calls=%async_computation | async-start | bytes 6291456 | tf_op jit(solution)/shard_map/all_to_all | solution.py:47
  306.7 37.6 %all-to-all-done = bf16[8,768,256]{2,1,0:T(8,128)(2,1)} async-done(((bf16[8,768,256]{2,1,0:T(8,128)(2,1)}), bf16[8,768,256]{2,1,0:T(8,128)(2,1)}, u32[]{:S(2)}, u32[]{:S(2)}) %all-to-all-start) | async-done | bytes 3145760 | tf_op jit(solution)/shard_map/all_to_all | solution.py:47
  344.3 2.4 convert_reduce_fusion
  346.7 2.0 add_convert_fusion
  (19 shorter events, 0.1 us)
Async XLA Ops:
  7.4 83.3 %copy-start = (bf16[256,2048]{1,0:T(8,128)(2,1)S(1)}, bf16[256,2048]{1,0:T(8,128)(2,1)}, u32[]{:S(2)}) copy-start(bf16[256,2048]{1,0:T(8,128)(2,1)} %param.15) | copy-start | bytes 3145732
  7.4 40.5 %all-gather.5.cloned.1.call-start = ((), (), s32[]{:S(2)}) async-start(), calls=%async_computation.1 | async-start | bytes 3538944 | tf_op jit(solution)/shard_map/all_gather | solution.py:59
  8.1 166.7 %all-reduce.2.cloned.1.call-start = ((), (), s32[]{:S(2)}) async-start(), calls=%async_computation.2 | async-start | bytes 6291456 | tf_op jit(solution)/shard_map/psum | solution.py:85
  47.9 3.4 copy-start.1
  51.2 33.2 %copy-start.5 = (bf16[2048,256]{1,0:T(8,128)(2,1)S(1)}, bf16[2048,256]{1,0:T(8,128)(2,1)}, u32[]{:S(2)}) copy-start(bf16[2048,256]{1,0:T(8,128)(2,1)} %param.11) | copy-start | bytes 3145732
  85.6 0.7 copy-start.7
  87.6 2.9 copy-start.4
  93.4 0.9 copy-start.2
  93.4 1.0 copy-start.3
  93.4 107.5 %all-gather.7.cloned.1.call-start = ((), (), s32[]{:S(2)}) async-start(), calls=%async_computation.3 | async-start | bytes 8650752 | tf_op jit(solution)/shard_map/all_gather | solution.py:36
  95.1 184.4 %all-gather.9.cloned.1.call-start = ((), (), s32[]{:S(2)}) async-start(), calls=%async_computation.4 | async-start | bytes 4325376 | tf_op jit(solution)/shard_map/all_gather | solution.py:95
  95.7 105.2 %copy-start.6 = (f32[2048]{0:T(1024)S(1)}, f32[2048]{0:T(1024)}, u32[]{:S(2)}) copy-start(f32[2048]{0:T(1024)} %param.16) | copy-start | bytes 24580
  298.1 46.2 %all-to-all-start = ((bf16[8,768,256]{2,1,0:T(8,128)(2,1)}), bf16[8,768,256]{2,1,0:T(8,128)(2,1)}, u32[]{:S(2)}, u32[]{:S(2)}) async-start(bf16[8,768,256]{2,1,0:T(8,128)(2,1)} %bitcast.57), calls=%async_computation | async-start | bytes 6291456 | tf_op jit(solution)/shard_map/all_to_all | solution.py:47
Sparse Core Ops, SparseCore 0:
  10.0 37.8 all-gather.4
  93.5 81.2 all-reduce.1
Sparse Core Ops, SparseCore 1:
  96.5 104.4 all-gather.6
  203.4 76.1 all-gather.8
where the time goes:
time: 356 us
  waiting for transfers between devices  246 us (69%)
  matrix products  38.1 us (11%)
  blocking collectives  30.5 us (9%)
  between operations  15 us (4%)
  other arithmetic  12.2 us (3%)
  starting transfers between devices  8.92 us (3%)
  local copies, waits for them, and re-layouts  5.37 us (2%)
    psum x1, waiting for transfers between devices, body(): lax.psum(partial_value.astype(jnp.bfloat16), 'tp').astype(jnp.float32)  79.1 us
    all_gather x1, waiting for transfers between devices, body(): lax.all_gather(w_down, SEQ, axis=1, tiled=True)  69.3 us
    all_gather x1, waiting for transfers between devices, body(): features = lax.all_gather(tokens, 'tp', axis=1, tiled=True)  39.5 us
    all_to_all x1, waiting for transfers between devices, sum_at_owner(): lax.all_to_all(tiles, axis, split_axis=0, concat_axis=0, tiled=True)  37.6 us
    all_gather x2, blocking collectives, entering(): pieces = lax.all_gather(total.astype(jnp.bfloat16), axis)  30.5 us
    all_gather x1, waiting for transfers between devices, in_one_piece(): lax.all_gather(both, axis, axis=dim, tiled=True)  19.3 us
    dot_general x1, matrix products, body(): jnp.dot(hidden, lax.all_gather(w_down, SEQ, axis=1, tiled=True), preferre...  14.9 us
    dot_general x1, matrix products, body(): upward_sum = jnp.dot(ffn_in, pieces[1], preferred_element_type=jnp.float32)  9.24 us
  transfers between devices with their start and end apart: 5, of which 5 were waited for; matrix products, arithmetic and copies ran while one was open for 5% of the time, Pallas kernels for 0%

commit v1 on v0

--- a/solution.py
+++ b/solution.py
@@ -1,3 +1,4 @@
+import functools
 import jax
 import jax.numpy as jnp
 from jax import lax
@@ -6,6 +7,22 @@
 
 HD = 128
 SEQ = ("seq_0", "seq_1")
+
+
+def form_the_types(local_values, device_axis):
+    inter = jnp.concatenate(
+        lax.all_to_all(
+            jnp.stack([local_values for _ in range(lax.axis_size(device_axis))], axis=0),
+            split_axis=0,
+            axis_name=device_axis,
+            concat_axis=0,
+        ),
+        axis=1,
+    )
+    return inter
+
+
+order_the_slots = functools.partial(form_the_types, device_axis=SEQ)
 
 
 def nothing_yet(array, identity):
@@ -91,9 +108,7 @@
     gate_sum = jnp.dot(ffn_in, pieces[0], preferred_element_type=jnp.float32)
     upward_sum = jnp.dot(ffn_in, pieces[1], preferred_element_type=jnp.float32)
     hidden = (jax.nn.silu(gate_sum) * upward_sum).astype(jnp.bfloat16)
-    terms = jnp.dot(
-        hidden, lax.all_gather(w_down, SEQ, axis=1, tiled=True), preferred_element_type=jnp.float32
-    )
+    terms = jnp.dot(hidden, order_the_slots(w_down), preferred_element_type=jnp.float32)
     mlp_share = sum_at_owner(terms.astype(jnp.bfloat16), "tp", 1)
     return (resid + mlp_share).astype(jnp.bfloat16)
 

time: 356 us -> 332 us (0.933)
  waiting for transfers between devices: 246 us -> 214 us
  starting transfers between devices: 8.92 us -> 13.2 us
    all_gather x1 -> x0, waiting for transfers between devices: 69.3 us -> none  [body(): lax.all_gather(w_down, SEQ, axis=1, tiled=True)]
    all_gather x1, waiting for transfers between devices: 19.3 us -> 67.8 us  [in_one_piece(): lax.all_gather(both, axis, axis=dim, tiled=True)]
    psum x1, waiting for transfers between devices: 79.1 us -> 68.9 us  [body(): lax.psum(partial_value.astype(jnp.bfloat16), 'tp').astype(jnp.float32)]
    all_to_all x0 -> x1, starting transfers between devices: none -> 8.33 us  [form_the_types(): lax.all_to_all(jnp.stack([local_values for _ in range(lax.axis_size(devic...]
    all_to_all x1, starting transfers between devices: 8.61 us -> 4.82 us  [sum_at_owner(): lax.all_to_all(tiles, axis, split_axis=0, concat_axis=0, tiled=True)]
  transfers between devices with their start and end apart: 5 -> 5, of which waited for: 5 -> 4; matrix products, arithmetic and copies ran while one was open for 5% -> 6% of each run, Pallas kernels for 0% -> 0%
where the time goes in v1:
time: 332 us; the launch traced here: 331 us
  waiting for transfers between devices  214 us (64%)
  matrix products  38 us (11%)
  blocking collectives  30.5 us (9%)
  between operations  15 us (5%)
  starting transfers between devices  13.2 us (4%)
  other arithmetic  12 us (4%)
  local copies, waits for them, and re-layouts  7.94 us (2%)
    psum x1, waiting for transfers between devices, body(): lax.psum(partial_value.astype(jnp.bfloat16), 'tp').astype(jnp.float32)  68.9 us
    all_gather x1, waiting for transfers between devices, in_one_piece(): lax.all_gather(both, axis, axis=dim, tiled=True)  67.8 us
    all_gather x1, waiting for transfers between devices, body(): features = lax.all_gather(tokens, 'tp', axis=1, tiled=True)  39.5 us
    all_to_all x1, waiting for transfers between devices, sum_at_owner(): lax.all_to_all(tiles, axis, split_axis=0, concat_axis=0, tiled=True)  37.6 us
    all_gather x2, blocking collectives, entering(): pieces = lax.all_gather(total.astype(jnp.bfloat16), axis)  30.5 us
    dot_general x1, matrix products, body(): jnp.dot(hidden, order_the_slots(w_down), preferred_element_type=jnp.float32)  14.8 us
    dot_general x1, matrix products, body(): upward_sum = jnp.dot(ffn_in, pieces[1], preferred_element_type=jnp.float32)  9.17 us
    all_to_all x1, starting transfers between devices, form_the_types(): lax.all_to_all(jnp.stack([local_values for _ in range(lax.axis_size(devic...  8.33 us
  transfers between devices with their start and end apart: 5, of which 4 were waited for; matrix products, arithmetic and copies ran while one was open for 6% of the time, Pallas kernels for 0%

profile of v1, /device:TPU:1, one launch (start us, length us, event | category | flops | bytes accessed | tf_op | source)
XLA Modules:
  0.0 331.1 jit_solution(11919737368756402043)
XLA Ops:
  7.4 0.7 all-gather.4.cloned.1.call-update
  8.1 0.0 all-reduce.2.cloned.1.call-start
  8.2 0.2 iota_compare_fusion
  8.3 39.5 %all-gather.4.cloned.1.call-done = bf16[768,2048]{1,0:T(8,128)(2,1)} async-done(((bf16[768,256]{1,0:T(8,128)(2,1)}), bf16[768,2048]{1,0:T(8,128)(2,1)}) %all-gather.4.cloned.1.call-update) | async-done | bytes 3145744 | tf_op jit(solution)/shard_map/all_gather | solution.py:76
  47.9 3.3 %convolution_convert_fusion.2 = bf16[768,256]{0,1:T(8,128)(2,1)S(1)} fusion(bf16[768,2048]{1,0:T(8,128)(2,1)} %all-gather.4.cloned.1.call-done, bf16[2048,256]{1,0:T(8,128)(2,1)} %param.12), kind=kOutput, calls=%fused_computation.20 | convolution fusion | flops 805502976 | bytes 4587520 | tf_op jit(solution)/shard_map/dot_general | solution.py:79
  51.2 2.4 convolution_convert_fusion.4
  53.6 0.3 convolution_convert_fusion.5
  53.9 20.8 %all-gather = bf16[16,128,128]{2,1,0:T(8,128)(2,1)S(1)} all-gather(bf16[2,128,128]{2,1,0:T(8,128)(2,1)S(1)} %convolution_convert_fusion.5), channel_id=2, replica_groups=mesh['seq_0'=4,'seq_1'=8,'tp'=8] {'seq_1'}, dimensions={0}, use_global_device_ids=true | all-gather | bytes 589824 | tf_op jit(solution)/shard_map/all_gather | solution.py:37
  74.7 0.1 fusion.28
  74.7 9.7 %all_gather.19 = bf16[4,2,128,128]{3,2,1,0:T(8,128)(2,1)S(1)} all-gather(bf16[1,2,128,128]{3,2,1,0:T(8,128)(2,1)S(1)} %fusion.28), channel_id=1, replica_groups=mesh['seq_0'=4,'seq_1'=8,'tp'=8] {'seq_0'}, dimensions={0}, use_global_device_ids=true | all-gather | bytes 327680 | tf_op jit(solution)/shard_map/all_gather | solution.py:37
  84.5 1.1 convolution_convert_fusion.3
  85.6 0.7 copy-done.8
  86.3 1.3 fusion.29
  87.6 2.9 multiply_reduce_fusion.1
  90.5 0.1 multiply_convert_fusion.2
  90.6 2.7 convolution_convert_fusion.1
  93.4 0.0 all-gather.6.cloned.1.call-start
  93.5 0.8 copy-done.3
  94.3 0.1 copy-done.4
  94.3 0.7 pad_maximum_fusion
  95.1 2.6 stack.2
  97.7 8.3 %all-to-all-start = ((bf16[32,1024,64]{1,2,0:T(8,128)(2,1)}), bf16[32,1024,64]{1,2,0:T(8,128)(2,1)}, u32[]{:S(2)}, u32[]{:S(2)}) async-start(bf16[32,1024,64]{1,2,0:T(8,128)(2,1)} %stack.2), calls=%async_computation | async-start | bytes 8388608 | tf_op jit(solution)/shard_map/all_to_all | solution.py:14
  106.0 68.9 %all-reduce.2.cloned.1.call-done = bf16[768,2048]{1,0:T(8,128)(2,1)} async-done(((bf16[768,2048]{1,0:T(8,128)(2,1)}), bf16[768,2048]{1,0:T(8,128)(2,1)}) %all-reduce.2.cloned.1.call-update) | async-done | bytes 3145744 | tf_op jit(solution)/shard_map/psum | solution.py:102
  174.9 6.5 %convert_add_fusion = (f32[768,2048]{1,0:T(8,128)}, f32[768]{0:T(1024)S(1)}) fusion(bf16[768,2048]{1,0:T(8,128)(2,1)} %all-reduce.2.cloned.1.call-done, bf16[768,2048]{1,0:T(8,128)(2,1)} %all-gather.4.cloned.1.call-done), kind=kLoop, calls=%fused_computation.3 | loop fusion | flops 7863552 | bytes 12585984 | tf_op jit(solution)/shard_map/add | solution.py:103
  181.4 67.8 %all-gather.6.cloned.1.call-done = bf16[2048,2048]{1,0:T(8,128)(2,1)} async-done(((bf16[64,2048]{1,0:T(8,128)(2,1)}), bf16[2048,2048]{1,0:T(8,128)(2,1)}) %all-gather.6.cloned.1.call-update) | async-done | bytes 8388624 | tf_op jit(solution)/shard_map/all_gather | solution.py:53
  249.2 9.2 %fusion = f32[768,1024]{1,0:T(8,128)} fusion(bf16[2048,2048]{1,0:T(8,128)(2,1)} %all-gather.6.cloned.1.call-done, f32[2048]{0:T(1024)S(1)} %copy-done.7, f32[768]{0:T(1024)S(1)} %add_rsqrt_fusion.1, bf16[768,2048]{1,0:T(8,128)(2,1)} %all-reduce.2.cloned.1.call-done, bf16[768,2048]{1,0:T(8,128)(2,1)} %all-gather.4.cloned.1.call-done), kind=kOutput, calls=%fused_computation.5 | convolution fusion | flops 3230662656 | bytes 13642752 | tf_op jit(solution)/shard_map/dot_general | solution.py:109
  258.3 14.8 %convolution_convert_fusion = bf16[768,2048]{1,0:T(8,128)(2,1)} fusion(bf16[1024,2048]{0,1:T(8,128)(2,1)} %bitcast.11, f32[768,1024]{1,0:T(8,128)} %fusion, bf16[2048,2048]{1,0:T(8,128)(2,1)} %all-gather.6.cloned.1.call-done, f32[2048]{0:T(1024)S(1)} %copy-done.7, f32[768]{0:T(1024)S(1)} %add_rsqrt_fusion.1, ...), kind=kOutput, calls=%fused_computation.9 | convolution fusion | flops 6458179584 | bytes 20982784 | tf_op jit(solution)/shard_map/dot_general | solution.py:111
  273.2 3.7 %copy.31 = bf16[96,8,8,256]{3,2,0,1:T(8,128)(2,1)} copy(bf16[96,8,8,256]{3,2,1,0:T(8,128)(2,1)} %bitcast.61) | data formatting | bytes 6291456 | tf_op jit(solution)/shard_map/reshape | solution.py:58
  276.9 4.8 %all-to-all-start.1 = ((bf16[8,768,256]{2,1,0:T(8,128)(2,1)}), bf16[8,768,256]{2,1,0:T(8,128)(2,1)}, u32[]{:S(2)}, u32[]{:S(2)}) async-start(bf16[8,768,256]{2,1,0:T(8,128)(2,1)} %bitcast.60), calls=%async_computation.1 | async-start | bytes 6291456 | tf_op jit(solution)/shard_map/all_to_all | solution.py:64
  281.7 37.6 %all-to-all-done.1 = bf16[8,768,256]{2,1,0:T(8,128)(2,1)} async-done(((bf16[8,768,256]{2,1,0:T(8,128)(2,1)}), bf16[8,768,256]{2,1,0:T(8,128)(2,1)}, u32[]{:S(2)}, u32[]{:S(2)}) %all-to-all-start.1) | async-done | bytes 3145760 | tf_op jit(solution)/shard_map/all_to_all | solution.py:64
  319.3 2.4 convert_reduce_fusion
  321.7 2.0 add_convert_fusion
  (21 shorter events, 0.1 us)
Async XLA Ops:
  7.4 83.3 %copy-start = (bf16[256,2048]{1,0:T(8,128)(2,1)S(1)}, bf16[256,2048]{1,0:T(8,128)(2,1)}, u32[]{:S(2)}) copy-start(bf16[256,2048]{1,0:T(8,128)(2,1)} %param.15) | copy-start | bytes 3145732
  7.4 40.5 %all-gather.4.cloned.1.call-start = ((), (), s32[]{:S(2)}) async-start(), calls=%async_computation.2 | async-start | bytes 3538944 | tf_op jit(solution)/shard_map/all_gather | solution.py:76
  8.1 166.8 %all-reduce.2.cloned.1.call-start = ((), (), s32[]{:S(2)}) async-start(), calls=%async_computation.3 | async-start | bytes 6291456 | tf_op jit(solution)/shard_map/psum | solution.py:102
  47.9 3.4 %copy-start.1 = (bf16[768,2048]{1,0:T(8,128)(2,1)S(1)}, bf16[768,2048]{1,0:T(8,128)(2,1)}, u32[]{:S(2)}) copy-start(bf16[768,2048]{1,0:T(8,128)(2,1)} %all-gather.4.cloned.1.call-done) | copy-start | bytes 9437188
  51.2 33.2 %copy-start.6 = (bf16[2048,256]{1,0:T(8,128)(2,1)S(1)}, bf16[2048,256]{1,0:T(8,128)(2,1)}, u32[]{:S(2)}) copy-start(bf16[2048,256]{1,0:T(8,128)(2,1)} %param.11) | copy-start | bytes 3145732
  85.6 0.7 copy-start.8
  87.6 2.9 copy-start.5
  93.4 0.9 copy-start.3
  93.4 1.0 copy-start.4
  93.4 1.7 copy-start.2
  93.4 155.8 %all-gather.6.cloned.1.call-start = ((), (), s32[]{:S(2)}) async-start(), calls=%async_computation.4 | async-start | bytes 8650752 | tf_op jit(solution)/shard_map/all_gather | solution.py:53
  97.7 160.7 %all-to-all-start = ((bf16[32,1024,64]{1,2,0:T(8,128)(2,1)}), bf16[32,1024,64]{1,2,0:T(8,128)(2,1)}, u32[]{:S(2)}, u32[]{:S(2)}) async-start(bf16[32,1024,64]{1,2,0:T(8,128)(2,1)} %stack.2), calls=%async_computation | async-start | bytes 8388608 | tf_op jit(solution)/shard_map/all_to_all | solution.py:14
  106.0 143.2 %copy-start.7 = (f32[2048]{0:T(1024)S(1)}, f32[2048]{0:T(1024)}, u32[]{:S(2)}) copy-start(f32[2048]{0:T(1024)} %param.16) | copy-start | bytes 24580
  276.9 42.4 %all-to-all-start.1 = ((bf16[8,768,256]{2,1,0:T(8,128)(2,1)}), bf16[8,768,256]{2,1,0:T(8,128)(2,1)}, u32[]{:S(2)}, u32[]{:S(2)}) async-start(bf16[8,768,256]{2,1,0:T(8,128)(2,1)} %bitcast.60), calls=%async_computation.1 | async-start | bytes 6291456 | tf_op jit(solution)/shard_map/all_to_all | solution.py:64
Sparse Core Ops, SparseCore 0:
  10.0 37.8 all-gather.3
  93.5 81.2 all-reduce.1
Sparse Core Ops, SparseCore 1:
  96.5 152.6 all-gather.5
